TPU v7x, 256 devices: a whole 4x4x8 slice. The times are simulated.
256 devices in a mesh: dev: 64 (over z, y, core), rep: 4 (over x).
Axes of the slice: x: 4, y: 4, z: 8, core: 2. Of those that a mesh axis runs over, the one named last changes fastest.
Arguments:
- features: bfloat16 [262144, 256], P(('dev', 'rep')), may hold values from -6 to 6
- history: bfloat16 [262144, 256], P(('dev', 'rep')), may hold values from -6 to 6
- new_owner: int32 [256, 64], P(('dev', 'rep')), may hold values from 0 to 63, as said below
- pull_rows: int32 [262144], P(('dev', 'rep')), may hold values from 0 to 1023
- occupancy: int32 [2048, 16], P(('dev', 'rep')), may hold values from 0 to 1, as said below
- adj_local: bfloat16 [262144, 1024], P(('dev', 'rep')), may hold values from -0.125 to 0.125
- adj_boundary: bfloat16 [262144, 1024], P(('dev', 'rep')), may hold values from -0.125 to 0.125
- w_first: bfloat16 [256, 256], replicated, may hold values from -0.375 to 0.375
- bias_first: float32 [256], replicated, may hold values from -3 to 3
- w_second: bfloat16 [256, 256], replicated, may hold values from -0.375 to 0.375
- cotangent: bfloat16 [262144, 256], P(('dev', 'rep')), may hold values from -24 to 24
Outputs:
- hidden: bfloat16 [262144, 256], P(('dev', 'rep'))
- output: bfloat16 [262144, 256], P(('dev', 'rep'))
- w_second_grad: float32 [256, 256], replicated
Inputs may be any that keep to these rules, and one draw needn't show every extreme that they name: Each row of new_owner is a permutation of 0 to 63. `occupancy`: tile flags of 0 or 1.
All inputs are finite; a program needn't handle non-finite values.
Results may differ from a plain program's by a relative error of at most 0.0061.
Values may be sent and summed in bfloat16 or wider, within the bound.
A program may use at most 64 MiB of HBM per device.

v0:
```python
import jax
import jax.numpy as jnp
from jax import lax
from jax.sharding import Mesh
from jax.sharding import PartitionSpec as P

DEV = ("dev_0", "dev_1", "dev_2")
DEV_REP = ("dev_0", "dev_1", "dev_2", "rep")


def in_one_piece(arrays, axis, split_dim, concat_dim, along):
    ends, at = ([], 0)
    for a in arrays[:-1]:
        at += a.shape[along]
        ends.append(at)
    both = jnp.concatenate(arrays, axis=along)
    return tuple(
        jnp.split(
            lax.all_to_all(both, axis, split_axis=split_dim, concat_axis=concat_dim, tiled=True),
            ends,
            axis=along,
        )
    )


def padded_to(lines, count):
    spare = -len(lines) % count
    return jnp.pad(lines, [(0, spare)] + [(0, 0)] * (lines.ndim - 1))


def copy_for_each(array, axis):
    copies = jnp.broadcast_to(array, (lax.axis_size(axis), *array.shape))
    return lax.all_to_all(copies, axis, split_axis=0, concat_axis=0, tiled=True)


def in_order(tiles, dim):
    dims = list(tiles.shape[1:])
    dims[dim] *= tiles.shape[0]
    return jnp.moveaxis(tiles, 0, dim).reshape(dims)


def whole_of(array, axes, dim):
    far, near = axes
    leading = copy_for_each(array, far)
    tiles = jnp.swapaxes(copy_for_each(leading, near), 0, 1)
    return in_order(tiles.reshape(-1, *array.shape), dim)


def split_up(array, dim, count):
    dims = array.shape
    tiles = array.reshape(*dims[:dim], count, dims[dim] // count, *dims[dim + 1 :])
    return jnp.moveaxis(tiles, dim, 0)


def summed_on_arrival(array, axis, dim):
    tiles = split_up(array, dim, lax.axis_size(axis))
    arrived = lax.all_to_all(tiles, axis, split_axis=0, concat_axis=0, tiled=True)
    return arrived.sum(axis=0)


def summed_rows(array, axes, dim):
    far, near = axes
    own = summed_on_arrival(split_up(array, dim, lax.axis_size(far)), near, dim + 1)
    return jnp.sum(lax.all_to_all(own, far, 0, 0, tiled=True), axis=0)


def nested_sum(array, axes):
    lines = array.reshape(-1, array.shape[-1])
    padded = padded_to(lines, lax.axis_size(axes[0]) * lax.axis_size(axes[1]))
    whole = whole_of(summed_rows(padded, axes, 0), axes, 0)
    return lax.slice_in_dim(whole, 0, len(lines)).reshape(array.shape)


def expand(occupied):
    return jnp.repeat(jnp.repeat(occupied, 128, axis=0), 128, axis=1).astype(jnp.bfloat16)


def dense_terms(owned, remote, adj_local, adj_boundary, occupancy):
    height = owned.shape[0]
    full_mask = expand(occupancy)
    local_tile = adj_local * full_mask[:, :height]
    edge_tile = adj_boundary * full_mask[:, height:]
    summed = jnp.dot(local_tile, owned, preferred_element_type=jnp.float32)
    summed = summed + jnp.dot(edge_tile, remote, preferred_element_type=jnp.float32)
    partial_value = lax.dot_general(
        edge_tile, owned, (((0,), (0,)), ((), ())), preferred_element_type=jnp.float32
    )
    return (summed, partial_value)


def body(
    features,
    history,
    new_owner,
    pull_rows,
    occupancy,
    adj_local,
    adj_boundary,
    w_first,
    bias_first,
    w_second,
    cotangent,
):
    peer_count = lax.axis_size(DEV)
    height, breadth = features.shape
    cluster = height // peer_count
    pulled = pull_rows.shape[0]
    per_peer = pulled // peer_count
    indices = jnp.arange(peer_count, dtype=jnp.int32)
    matches = (new_owner[0][:, None] == indices[None, :]).astype(jnp.int32)
    inverse = jnp.sum(matches * indices[:, None], axis=0)

    def arrange(values):
        return values.reshape(peer_count, cluster, breadth)[inverse]

    requests = lax.all_to_all(
        pull_rows.reshape(peer_count, per_peer), DEV, split_axis=0, concat_axis=0, tiled=True
    ).reshape(pulled)

    def fetch_rows(values):
        return values[requests].reshape(peer_count, per_peer, breadth)

    selector = (requests[None, :] == jnp.arange(height, dtype=jnp.int32)[:, None]).astype(
        jnp.bfloat16
    )

    def collect(received):
        return jnp.dot(
            selector, received.reshape(pulled, breadth), preferred_element_type=jnp.float32
        )

    def layer_terms(owned, remote):
        return dense_terms(owned, remote, adj_local, adj_boundary, occupancy)

    moved_x, moved_h = in_one_piece((arrange(features), arrange(history)), DEV, 0, 0, 1)
    own_x = moved_x.reshape(height, breadth)
    own_h = moved_h.reshape(height, breadth)
    far_x, far_h = in_one_piece((fetch_rows(own_x), fetch_rows(own_h)), DEV, 0, 0, 1)
    summed_one, partial_one = layer_terms(own_x, far_x.reshape(pulled, breadth))
    pushed_one = lax.all_to_all(
        partial_one.astype(jnp.bfloat16).reshape(peer_count, per_peer, breadth),
        DEV,
        split_axis=0,
        concat_axis=0,
        tiled=True,
    )
    far_h = far_h.reshape(pulled, breadth)
    aggregate_one = (summed_one + collect(pushed_one)).astype(jnp.bfloat16)
    hidden = jnp.maximum(
        jnp.dot(aggregate_one, w_first, preferred_element_type=jnp.float32) + bias_first, 0.0
    ).astype(jnp.bfloat16)
    summed_two, partial_two = layer_terms(hidden, far_h)
    pushed_two = lax.all_to_all(
        partial_two.astype(jnp.bfloat16).reshape(peer_count, per_peer, breadth),
        DEV,
        split_axis=0,
        concat_axis=0,
        tiled=True,
    )
    aggregate_two = (summed_two + collect(pushed_two)).astype(jnp.bfloat16)
    output = jnp.dot(aggregate_two, w_second, preferred_element_type=jnp.float32).astype(
        jnp.bfloat16
    )
    local_grad = lax.dot_general(
        aggregate_two, cotangent, (((0,), (0,)), ((), ())), preferred_element_type=jnp.float32
    )
    gradient = nested_sum(local_grad, (("dev_0", "dev_1"), ("dev_2", "rep")))
    return (hidden, output, gradient)


def solution(mesh):
    finer = Mesh(
        mesh.devices.reshape(8, 4, 2, mesh.shape["rep"]), ("dev_0", "dev_1", "dev_2", "rep")
    )
    return jax.shard_map(
        body,
        mesh=finer,
        in_specs=(
            P(DEV_REP, None),
            P(DEV_REP, None),
            P(DEV_REP, None),
            P(DEV_REP),
            P(DEV_REP, None),
            P(DEV_REP, None),
            P(DEV_REP, None),
            P(),
            P(),
            P(),
            P(DEV_REP, None),
        ),
        out_specs=(P(DEV_REP, None), P(DEV_REP, None), P()),
        check_vma=False,
    )
```

profile of v0, /device:TPU:1, one launch (start us, length us, event | category | flops | bytes accessed | tf_op | source)
XLA Modules:
  0.0 208.1 jit_solution(64594992855767647)
XLA Ops:
  2.1 13.1 %all-to-all-start.1 = ((s32[64,1,16]{2,1,0:T(1,128)}), s32[64,1,16]{2,1,0:T(1,128)S(1)}, u32[]{:S(2)}, u32[]{:S(2)}) async-start(s32[64,1,16]{2,1,0:T(1,128)} %bitcast.7), calls=%async_computation.1 | async-start | bytes 65536 | tf_op jit(solution)/shard_map/all_to_all | solution.py:116
  19.4 5.2 %all-to-all-done.1 = s32[64,1,16]{2,1,0:T(1,128)S(1)} async-done(((s32[64,1,16]{2,1,0:T(1,128)}), s32[64,1,16]{2,1,0:T(1,128)S(1)}, u32[]{:S(2)}, u32[]{:S(2)}) %all-to-all-start.1) | async-done | bytes 4128 | tf_op jit(solution)/shard_map/all_to_all | solution.py:116
  24.6 5.1 %all-to-all-start = ((bf16[64,32,256]{2,1,0:T(8,128)(2,1)}), bf16[64,32,256]{2,1,0:T(8,128)(2,1)S(1)}, u32[]{:S(2)}, u32[]{:S(2)}) async-start(bf16[64,32,256]{2,1,0:T(8,128)(2,1)} %pad_maximum_fusion), calls=%async_computation | async-start | bytes 2097152 | tf_op jit(solution)/shard_map/all_to_all | solution.py:19
  31.1 26.8 %all-to-all-done = bf16[64,32,256]{2,1,0:T(8,128)(2,1)S(1)} async-done(((bf16[64,32,256]{2,1,0:T(8,128)(2,1)}), bf16[64,32,256]{2,1,0:T(8,128)(2,1)S(1)}, u32[]{:S(2)}, u32[]{:S(2)}) %all-to-all-start) | async-done | bytes 1048608 | tf_op jit(solution)/shard_map/all_to_all | solution.py:19
  57.9 3.9 %gather_fusion.3 = bf16[1024,256]{1,0:T(8,128)(2,1)S(1)} fusion(bf16[1024,256]{1,0:T(8,128)(2,1)S(1)} %bitcast.59, s32[1024]{0:T(1024)S(1)} %broadcast_clamp_fusion), kind=kCustom, calls=%fused_computation.3 | custom fusion | bytes 1052672 | tf_op jit(solution)/shard_map/gather | solution.py:121
  61.9 3.9 %gather_fusion.2 = bf16[1024,256]{1,0:T(8,128)(2,1)S(1)} fusion(bf16[1024,256]{1,0:T(8,128)(2,1)S(1)} %bitcast.56, s32[1024]{0:T(1024)S(1)} %broadcast_clamp_fusion), kind=kCustom, calls=%fused_computation.2 | custom fusion | bytes 1052672 | tf_op jit(solution)/shard_map/gather | solution.py:121
  67.0 6.5 %all-to-all-start.2 = ((bf16[64,32,256]{2,1,0:T(8,128)(2,1)}), bf16[64,32,256]{2,1,0:T(8,128)(2,1)}, u32[]{:S(2)}, u32[]{:S(2)}) async-start(bf16[64,32,256]{2,1,0:T(8,128)(2,1)} %pad_maximum_fusion.1), calls=%async_computation.2 | async-start | bytes 2097152 | tf_op jit(solution)/shard_map/all_to_all | solution.py:19
  73.6 4.5 %broadcast_in_dim.9 = bf16[1024,16,128]{2,1,0:T(8,128)(2,1)S(1)} broadcast(bf16[1024,16]{1,0:T(8,128)(2,1)S(1)} %bitcast.68), dimensions={0,1} | broadcast | bytes 4227072 | tf_op jit(solution)/shard_map/broadcast_in_dim | solution.py:75
  78.0 2.2 %copy.28 = bf16[128,8,16,128]{3,1,2,0:T(8,128)(2,1)S(1)} copy(bf16[128,8,16,128]{3,2,1,0:T(8,128)(2,1)S(1)} %bitcast.60) | data formatting | bytes 8388608
  83.7 17.9 %all-to-all-done.2 = bf16[64,32,256]{2,1,0:T(8,128)(2,1)} async-done(((bf16[64,32,256]{2,1,0:T(8,128)(2,1)}), bf16[64,32,256]{2,1,0:T(8,128)(2,1)}, u32[]{:S(2)}, u32[]{:S(2)}) %all-to-all-start.2) | async-done | bytes 1048608 | tf_op jit(solution)/shard_map/all_to_all | solution.py:19
  101.6 6.5 %all-to-all-start.3 = ((bf16[64,16,256]{2,1,0:T(8,128)(2,1)}), bf16[64,16,256]{2,1,0:T(8,128)(2,1)}, u32[]{:S(2)}, u32[]{:S(2)}) async-start(bf16[64,16,256]{2,1,0:T(8,128)(2,1)} %bitcast.70), calls=%async_computation.3 | async-start | bytes 1048576 | tf_op jit(solution)/shard_map/all_to_all | solution.py:140
  108.1 2.9 %fusion.11 = f32[1024,256]{1,0:T(8,128)S(1)} fusion(bf16[1024,256]{1,0:T(8,128)(2,1)S(1)} %bitcast.58, bf16[1024,1024]{1,0:T(8,128)(2,1)} %param.16, bf16[1024,2048]{1,0:T(8,128)(2,1)} %bitcast.62), kind=kOutput, calls=%fused_computation.28 | convolution fusion | flops 537919488 | bytes 5767168 | tf_op jit(solution)/shard_map/dot_general | solution.py:83
  114.1 11.6 %all-to-all-done.3 = bf16[64,16,256]{2,1,0:T(8,128)(2,1)} async-done(((bf16[64,16,256]{2,1,0:T(8,128)(2,1)}), bf16[64,16,256]{2,1,0:T(8,128)(2,1)}, u32[]{:S(2)}, u32[]{:S(2)}) %all-to-all-start.3) | async-done | bytes 524320 | tf_op jit(solution)/shard_map/all_to_all | solution.py:140
  125.6 3.2 %fusion.7 = bf16[1024,256]{1,0:T(8,128)(2,1)} fusion(bf16[256,256]{1,0:T(8,128)(2,1)S(1)} %copy-done.6, f32[1024,256]{1,0:T(8,128)} %convolution_add_fusion.2, bf16[1024,256]{1,0:T(8,128)(2,1)} %bitcast.14, s32[1024]{0:T(1024)S(1)} %eq.34, f32[256]{0:T(256)S(1)} %copy-done.7), kind=kOutput, calls=%fused_computation.18 | convolution fusion | flops 673447936 | bytes 2233344 | tf_op jit(solution)/shard_map/dot_general | solution.py:150
  128.9 2.6 %convolution_convert_fusion.1 = bf16[1024,256]{1,0:T(8,128)(2,1)} fusion(bf16[1024,1024]{1,0:T(8,128)(2,1)S(1)} %slice_multiply_fusion, bf16[1024,256]{1,0:T(8,128)(2,1)} %fusion.7), kind=kOutput, calls=%fused_computation.22 | convolution fusion | flops 537133056 | bytes 3145728 | tf_op jit(solution)/shard_map/dot_general | solution.py:85
  131.5 5.9 %all-to-all-start.4 = ((bf16[64,16,256]{2,1,0:T(8,128)(2,1)}), bf16[64,16,256]{2,1,0:T(8,128)(2,1)}, u32[]{:S(2)}, u32[]{:S(2)}) async-start(bf16[64,16,256]{2,1,0:T(8,128)(2,1)} %bitcast.71), calls=%async_computation.4 | async-start | bytes 1048576 | tf_op jit(solution)/shard_map/all_to_all | solution.py:153
  137.3 3.0 %fusion.10 = f32[1024,256]{1,0:T(8,128)S(1)} fusion(bf16[1024,256]{1,0:T(8,128)(2,1)} %fusion.7, bf16[1024,1024]{1,0:T(8,128)(2,1)} %param.16, bf16[1024,2048]{1,0:T(8,128)(2,1)} %bitcast.63), kind=kOutput, calls=%fused_computation.27 | convolution fusion | flops 537919488 | bytes 5767168 | tf_op jit(solution)/shard_map/dot_general | solution.py:83
  142.1 12.9 %all-to-all-done.4 = bf16[64,16,256]{2,1,0:T(8,128)(2,1)} async-done(((bf16[64,16,256]{2,1,0:T(8,128)(2,1)}), bf16[64,16,256]{2,1,0:T(8,128)(2,1)}, u32[]{:S(2)}, u32[]{:S(2)}) %all-to-all-start.4) | async-done | bytes 524320 | tf_op jit(solution)/shard_map/all_to_all | solution.py:153
  154.9 2.2 %fusion.8 = bf16[1024,256]{1,0:T(8,128)(2,1)S(1)} fusion(f32[1024,256]{1,0:T(8,128)} %convolution_add_fusion.1, bf16[1024,256]{1,0:T(8,128)(2,1)} %bitcast.17, s32[1024]{0:T(1024)S(1)} %eq.34), kind=kOutput, calls=%fused_computation.20 | convolution fusion | flops 538443776 | bytes 2101248 | tf_op jit(solution)/shard_map/dot_general | solution.py:128
  157.6 11.0 %all_to_all.52 = f32[8,32,1,256]{3,1,2,0:T(8,128)S(1)} all-to-all(f32[8,32,1,256]{3,1,2,0:T(8,128)S(1)} %bitcast.69), channel_id=1, replica_groups=mesh['dev_0'=8,'dev_1'=4,'dev_2'=2,'rep'=4] {'dev_2','rep'}, dimensions={0} | all-to-all | bytes 524288 | tf_op jit(solution)/shard_map/all_to_all | solution.py:57
  168.7 13.4 %all_to_all.53 = f32[32,1,256]{2,1,0:T(1,128)S(1)} all-to-all(f32[32,1,256]{2,1,0:T(1,128)S(1)} %reduce_sum.34), channel_id=1, replica_groups=mesh['dev_0'=8,'dev_1'=4,'dev_2'=2,'rep'=4] {'dev_0','dev_1'}, dimensions={0} | all-to-all | bytes 65536 | tf_op jit(solution)/shard_map/all_to_all | solution.py:64
  182.1 11.6 %all_to_all.54 = f32[32,1,256]{2,1,0:T(1,128)S(1)} all-to-all(f32[32,1,256]{2,1,0:T(1,128)S(1)} %broadcast_in_dim.10), channel_id=1, replica_groups=mesh['dev_0'=8,'dev_1'=4,'dev_2'=2,'rep'=4] {'dev_0','dev_1'}, dimensions={0} | all-to-all | bytes 65536 | tf_op jit(solution)/shard_map/all_to_all | solution.py:33
  194.5 6.2 %all-to-all-start.8 = ((f32[8,32,1,256]{3,1,2,0:T(8,128)}), f32[8,32,1,256]{3,1,2,0:T(8,128)S(1)}, u32[]{:S(2)}, u32[]{:S(2)}) async-start(f32[8,32,1,256]{3,1,2,0:T(8,128)} %broadcast_in_dim.11), calls=%async_computation.8 | async-start | bytes 524288 | tf_op jit(solution)/shard_map/all_to_all | solution.py:33
  201.7 5.5 %all-to-all-done.8 = f32[8,32,1,256]{3,1,2,0:T(8,128)S(1)} async-done(((f32[8,32,1,256]{3,1,2,0:T(8,128)}), f32[8,32,1,256]{3,1,2,0:T(8,128)S(1)}, u32[]{:S(2)}, u32[]{:S(2)}) %all-to-all-start.8) | async-done | bytes 262176 | tf_op jit(solution)/shard_map/all_to_all | solution.py:33
  (48 shorter events, 19.7 us)
Async XLA Ops:
  0.6 15.4 %copy-start = (bf16[1024,256]{1,0:T(8,128)(2,1)S(1)}, bf16[1024,256]{1,0:T(8,128)(2,1)}, u32[]{:S(2)}) copy-start(bf16[1024,256]{1,0:T(8,128)(2,1)} %param.12) | copy-start | bytes 1572868
  2.1 22.5 %all-to-all-start.1 = ((s32[64,1,16]{2,1,0:T(1,128)}), s32[64,1,16]{2,1,0:T(1,128)S(1)}, u32[]{:S(2)}, u32[]{:S(2)}) async-start(s32[64,1,16]{2,1,0:T(1,128)} %bitcast.7), calls=%async_computation.1 | async-start | bytes 65536 | tf_op jit(solution)/shard_map/all_to_all | solution.py:116
  24.6 33.3 %all-to-all-start = ((bf16[64,32,256]{2,1,0:T(8,128)(2,1)}), bf16[64,32,256]{2,1,0:T(8,128)(2,1)S(1)}, u32[]{:S(2)}, u32[]{:S(2)}) async-start(bf16[64,32,256]{2,1,0:T(8,128)(2,1)} %pad_maximum_fusion), calls=%async_computation | async-start | bytes 2097152 | tf_op jit(solution)/shard_map/all_to_all | solution.py:19
  65.8 7.6 %copy-start.5 = (s32[8,16]{1,0:T(8,128)S(1)}, s32[8,16]{1,0:T(8,128)}, u32[]{:S(2)}) copy-start(s32[8,16]{1,0:T(8,128)} %param.15) | copy-start | bytes 1540
  67.0 34.6 %all-to-all-start.2 = ((bf16[64,32,256]{2,1,0:T(8,128)(2,1)}), bf16[64,32,256]{2,1,0:T(8,128)(2,1)}, u32[]{:S(2)}, u32[]{:S(2)}) async-start(bf16[64,32,256]{2,1,0:T(8,128)(2,1)} %pad_maximum_fusion.1), calls=%async_computation.2 | async-start | bytes 2097152 | tf_op jit(solution)/shard_map/all_to_all | solution.py:19
  78.0 2.2 %copy-start.2 = (bf16[1024,1024]{1,0:T(8,128)(2,1)S(1)}, bf16[1024,1024]{1,0:T(8,128)(2,1)}, u32[]{:S(2)}) copy-start(bf16[1024,1024]{1,0:T(8,128)(2,1)} %param.17) | copy-start | bytes 6291460
  80.2 1.9 copy-start.1
  101.6 24.1 %all-to-all-start.3 = ((bf16[64,16,256]{2,1,0:T(8,128)(2,1)}), bf16[64,16,256]{2,1,0:T(8,128)(2,1)}, u32[]{:S(2)}, u32[]{:S(2)}) async-start(bf16[64,16,256]{2,1,0:T(8,128)(2,1)} %bitcast.70), calls=%async_computation.3 | async-start | bytes 1048576 | tf_op jit(solution)/shard_map/all_to_all | solution.py:140
  112.3 13.3 %copy-start.6 = (bf16[256,256]{1,0:T(8,128)(2,1)S(1)}, bf16[256,256]{1,0:T(8,128)(2,1)}, u32[]{:S(2)}) copy-start(bf16[256,256]{1,0:T(8,128)(2,1)} %param.18) | copy-start | bytes 393220
  112.4 13.3 %copy-start.7 = (f32[256]{0:T(256)S(1)}, f32[256]{0:T(256)}, u32[]{:S(2)}) copy-start(f32[256]{0:T(256)} %param.19) | copy-start | bytes 3076
  131.5 23.5 %all-to-all-start.4 = ((bf16[64,16,256]{2,1,0:T(8,128)(2,1)}), bf16[64,16,256]{2,1,0:T(8,128)(2,1)}, u32[]{:S(2)}, u32[]{:S(2)}) async-start(bf16[64,16,256]{2,1,0:T(8,128)(2,1)} %bitcast.71), calls=%async_computation.4 | async-start | bytes 1048576 | tf_op jit(solution)/shard_map/all_to_all | solution.py:153
  142.1 15.1 %copy-start.3 = (bf16[1024,256]{1,0:T(8,128)(2,1)S(1)}, bf16[1024,256]{1,0:T(8,128)(2,1)}, u32[]{:S(2)}) copy-start(bf16[1024,256]{1,0:T(8,128)(2,1)} %param.21) | copy-start | bytes 1572868
  157.2 43.5 %copy-start.4 = (bf16[256,256]{1,0:T(8,128)(2,1)S(1)}, bf16[256,256]{1,0:T(8,128)(2,1)}, u32[]{:S(2)}) copy-start(bf16[256,256]{1,0:T(8,128)(2,1)} %param.20) | copy-start | bytes 393220
  194.5 12.8 %all-to-all-start.8 = ((f32[8,32,1,256]{3,1,2,0:T(8,128)}), f32[8,32,1,256]{3,1,2,0:T(8,128)S(1)}, u32[]{:S(2)}, u32[]{:S(2)}) async-start(f32[8,32,1,256]{3,1,2,0:T(8,128)} %broadcast_in_dim.11), calls=%async_computation.8 | async-start | bytes 524288 | tf_op jit(solution)/shard_map/all_to_all | solution.py:33
where the time goes:
time: 209 us; the launch traced here: 208 us
  waiting for transfers between devices  79.8 us (38%)
  starting transfers between devices  43.3 us (21%)
  blocking collectives  36 us (17%)
  local copies, waits for them, and re-layouts  23.7 us (11%)
  matrix products  20.3 us (10%)
  other arithmetic  4.08 us (2%)
    all_to_all x2, waiting for transfers between devices, in_one_piece(): lax.all_to_all(both, axis, split_axis=split_dim, concat_axis=concat_dim,...  44.7 us
    all_to_all x1, blocking collectives, summed_rows(): return jnp.sum(lax.all_to_all(own, far, 0, 0, tiled=True), axis=0)  13.4 us
    all_to_all x1, starting transfers between devices, body(): lax.all_to_all(pull_rows.reshape(peer_count, per_peer), DEV, split_axis=0...  13.1 us
    all_to_all x1, waiting for transfers between devices, body(): lax.all_to_all(partial_two.astype(jnp.bfloat16).reshape(peer_count, per_p...  12.9 us
    all_to_all x1, blocking collectives, copy_for_each(): return lax.all_to_all(copies, axis, split_axis=0, concat_axis=0, tiled=True)  11.6 us
    all_to_all x2, starting transfers between devices, in_one_piece(): lax.all_to_all(both, axis, split_axis=split_dim, concat_axis=concat_dim,...  11.6 us
    all_to_all x1, waiting for transfers between devices, body(): lax.all_to_all(partial_one.astype(jnp.bfloat16).reshape(peer_count, per_p...  11.6 us
    all_to_all x1, blocking collectives, summed_on_arrival(): lax.all_to_all(tiles, axis, split_axis=0, concat_axis=0, tiled=True)  11 us
  transfers between devices with their start and end apart: 6, of which 6 were waited for; matrix products, arithmetic and copies ran while one was open for 12% of the time, Pallas kernels for 0%

commit v1 on v0

v1 whole, which is shorter than its diff:
```python
import functools

import jax
import jax.numpy as jnp
from jax import lax
from jax.experimental import pallas as pl
from jax.experimental.pallas import tpu as pltpu
from jax.sharding import PartitionSpec as P

MESH = pl.DeviceIdType.MESH
F32, BF16, I32 = jnp.float32, jnp.bfloat16, jnp.int32

REQ, MIG_X, MIG_H, PULL_X, PUSH_1, PULL_H, PUSH_2, GRAD_A, GRAD_B, GRAD_C = range(10)


def iota(shape, dim):
    return lax.broadcasted_iota(I32, shape, dim)


def ones_where(condition):
    return jnp.where(condition, 1.0, 0.0).astype(BF16)


def dot(a, b):
    return jnp.dot(a, b, preferred_element_type=F32)


def step_kernel(
    n_dev,
    n_rep,
    n_y,
    n_core,
    features,
    history,
    owner_ref,
    pull_ref,
    occ_ref,
    adj_local,
    adj_boundary,
    w_first,
    bias_first,
    w_second,
    cotangent,
    hidden_out,
    output_out,
    grad_out,
    x_in,
    h_in,
    local,
    edge,
    edge_t,
    w1,
    w2,
    cot,
    cot_t,
    send_x,
    send_h,
    own_x,
    own_h,
    asked,
    asked_flat,
    sel,
    sel_t,
    occ_rows,
    fetch_x,
    fetch_h,
    part_1,
    part_2,
    far_x,
    far_h,
    push_1,
    push_2,
    acc,
    hidden,
    agg,
    result,
    grad,
    grad_in,
    slab_sum,
    line_in,
    total,
    grad_all,
    load_sem,
    store_sem,
    send_sem,
    recv_sem,
):
    me, rep = lax.axis_index("dev"), lax.axis_index("rep")
    rows, breadth = x_in.shape
    per_peer = rows // n_dev
    per_z = n_y * n_core
    slab = per_z * n_rep
    n_z = n_dev // per_z
    chunk = breadth // slab
    my_z, my_yc = me // per_z, me % per_z
    my_slab = my_yc * n_rep + rep
    step = 256

    def dev_peer(i):
        return lax.rem(me + i, n_dev)

    def slab_peer(i):
        return lax.rem(my_slab + i, slab)

    def slab_id(q):
        return (my_z * per_z + q // n_rep, q % n_rep)

    def each(count, body):
        def run(i, carry):
            body(i)
            return carry

        lax.fori_loop(1, count, run, 0)

    barrier = pltpu.get_barrier_semaphore()

    def greet(device):
        pl.semaphore_signal(barrier, inc=1, device_id=device, device_id_type=MESH)

    each(n_dev, lambda i: greet((dev_peer(i), rep)))

    def greet_across(i):
        r = lax.rem(rep + i, n_rep)

        def run(j, carry):
            greet((my_z * per_z + j, r))
            return carry

        lax.fori_loop(0, per_z, run, 0)

    each(n_rep, greet_across)

    loads = [
        pltpu.make_async_copy(src, dst, load_sem.at[k])
        for k, (src, dst) in enumerate(
            [
                (features, x_in),
                (history, h_in),
                (adj_local, local),
                (adj_boundary, edge),
                (cotangent, cot),
                (w_first, w1),
                (w_second, w2),
            ]
        )
    ]
    for load in loads:
        load.start()

    owners = jnp.broadcast_to(owner_ref[...], (8, n_dev)).astype(F32).astype(BF16)
    spread = ones_where(iota((n_dev, rows), 0) == iota((n_dev, rows), 1) // per_peer)
    target = dot(owners, spread)[0:1].astype(I32) * per_peer + iota((1, rows), 1) % per_peer
    loads[0].wait()
    loads[1].wait()

    def arrange(i, carry):
        at = pl.ds(pl.multiple_of(i * step, step), step)
        pick = ones_where(iota((step, rows), 0) + i * step == target)
        send_x[at] = dot(pick, x_in[...]).astype(BF16)
        send_h[at] = dot(pick, h_in[...]).astype(BF16)
        return carry

    lax.fori_loop(0, rows // step, arrange, 0)

    def block(d):
        return pl.ds(pl.multiple_of(d * per_peer, per_peer), per_peer)

    own_x[block(me)] = send_x[block(me)]
    own_h[block(me)] = send_h[block(me)]
    asked[me] = pull_ref[me // per_z]

    pl.semaphore_wait(barrier, n_dev - 1 + (n_rep - 1) * per_z)

    def remote(src, dst, stage, device):
        pltpu.make_async_remote_copy(
            src_ref=src,
            dst_ref=dst,
            send_sem=send_sem.at[stage],
            recv_sem=recv_sem.at[stage],
            device_id=device,
            device_id_type=MESH,
        ).start()

    def send_requests(i):
        peer = dev_peer(i)
        remote(pull_ref.at[peer // per_z], asked.at[me], REQ, (peer, rep))

    def exchange(src, dst, stage):
        def one(i):
            peer = dev_peer(i)
            remote(src.at[block(peer)], dst.at[block(me)], stage, (peer, rep))

        each(n_dev, one)

    others = pl.ds(0, rows - per_peer)

    def landed(dst, stage):
        pltpu.make_async_copy(dst.at[others], dst.at[others], recv_sem.at[stage]).wait()

    def left(src, stage):
        pltpu.make_async_copy(src.at[others], src.at[others], send_sem.at[stage]).wait()

    each(n_dev, send_requests)
    exchange(send_x, own_x, MIG_X)
    exchange(send_h, own_h, MIG_H)

    n_tiles = 2 * rows // 128
    tile_of = ones_where(iota((n_tiles, 2 * rows), 0) == iota((n_tiles, 2 * rows), 1) // 128)
    occ_rows[...] = dot(occ_ref[...].astype(F32).astype(BF16), tile_of)
    loads[2].wait()
    loads[3].wait()

    def mask_rows(i, carry):
        at = pl.ds(pl.multiple_of(i * 128, 128), 128)
        there = occ_rows[pl.ds(i, 1), :]
        flags = jnp.broadcast_to(there, (128, 2 * rows)).astype(BF16)
        local[at] = local[at] * flags[:, :rows]
        kept = edge[at] * flags[:, rows:]
        edge[at] = kept
        edge_t[:, at] = kept.T
        return carry

    lax.fori_loop(0, rows // 128, mask_rows, 0)

    pltpu.make_async_copy(
        asked.at[pl.ds(0, n_dev - 1)], asked.at[pl.ds(0, n_dev - 1)], recv_sem.at[REQ]
    ).wait()
    for d in range(n_dev):
        asked_flat[d : d + 1, :] = asked[d]
    first = (me % per_z) * per_peer
    wanted = asked_flat[...]
    high = (wanted // per_peer).astype(F32).astype(BF16)
    low = (wanted % per_peer).astype(F32).astype(BF16)
    widen = ones_where(iota((128, rows), 0) == first + iota((128, rows), 1) % per_peer)
    along = dot(high, widen) * per_peer + dot(low, widen)
    mine = iota((n_dev, rows), 0) == iota((n_dev, rows), 1) // per_peer
    as_row = jnp.sum(jnp.where(mine, along, 0.0), axis=0, keepdims=True).astype(I32)
    all_ones = jnp.ones((128, 128), BF16)

    def select(i, carry):
        at = pl.ds(pl.multiple_of(i * step, step), step)
        sel[at] = ones_where(iota((step, rows), 0) + i * step == as_row)
        entry = iota((step, n_dev), 0) + i * step
        take = ones_where(entry // per_peer == iota((step, n_dev), 1))
        here = iota((step, 128), 1) == first + iota((step, 128), 0) % per_peer
        hi = jnp.where(here, dot(take, high), 0.0).astype(BF16)
        lo = jnp.where(here, dot(take, low), 0.0).astype(BF16)
        as_column = (dot(hi, all_ones) * per_peer + dot(lo, all_ones)).astype(I32)
        for c in range(rows // 128):
            sel_t[at, c * 128 : (c + 1) * 128] = ones_where(as_column == iota((step, 128), 1) + c * 128)
        return carry

    lax.fori_loop(0, rows // step, select, 0)

    def product(dst, a, b):
        def run(i, carry):
            at = pl.ds(pl.multiple_of(i * step, step), step)
            dst[at] = dot(a[at], b[...]).astype(dst.dtype)
            return carry

        lax.fori_loop(0, a.shape[0] // step, run, 0)

    def add_product(dst, a, b):
        def run(i, carry):
            at = pl.ds(pl.multiple_of(i * step, step), step)
            dst[at] += dot(a[at], b[...])
            return carry

        lax.fori_loop(0, a.shape[0] // step, run, 0)

    landed(own_x, MIG_X)
    product(fetch_x, sel_t, own_x)
    exchange(fetch_x, far_x, PULL_X)
    product(part_1, edge_t, own_x)
    exchange(part_1, push_1, PUSH_1)
    far_x[block(me)] = fetch_x[block(me)]
    push_1[block(me)] = part_1[block(me)]
    product(acc, local, own_x)

    landed(own_h, MIG_H)
    product(fetch_h, sel_t, own_h)
    exchange(fetch_h, far_h, PULL_H)
    far_h[block(me)] = fetch_h[block(me)]
    loads[4].wait()
    cot_t[...] = cot[...].T
    loads[5].wait()
    loads[6].wait()

    landed(far_x, PULL_X)
    add_product(acc, edge, far_x)
    landed(push_1, PUSH_1)

    def to_hidden(i, carry):
        at = pl.ds(pl.multiple_of(i * step, step), step)
        gathered = (acc[at] + dot(sel[at], push_1[...])).astype(BF16)
        hidden[at] = jnp.maximum(dot(gathered, w1[...]) + bias_first[...], 0.0).astype(BF16)
        return carry

    lax.fori_loop(0, rows // step, to_hidden, 0)

    product(part_2, edge_t, hidden)
    exchange(part_2, push_2, PUSH_2)
    push_2[block(me)] = part_2[block(me)]
    hidden_store = pltpu.make_async_copy(hidden, hidden_out, store_sem.at[0])
    hidden_store.start()
    product(acc, local, hidden)
    landed(far_h, PULL_H)
    add_product(acc, edge, far_h)
    landed(push_2, PUSH_2)

    def to_agg(i, carry):
        at = pl.ds(pl.multiple_of(i * step, step), step)
        agg[at] = (acc[at] + dot(sel[at], push_2[...])).astype(BF16)
        return carry

    lax.fori_loop(0, rows // step, to_agg, 0)

    grad[...] = dot(cot_t[...], agg[...])

    def part_of(q):
        return pl.ds(pl.multiple_of(q * chunk, chunk), chunk)

    def scatter_grad(i):
        q = slab_peer(i)
        remote(grad.at[part_of(q)], grad_in.at[my_slab], GRAD_A, slab_id(q))

    each(slab, scatter_grad)
    grad_in[my_slab] = grad[part_of(my_slab)]
    product(result, agg, w2)
    output_store = pltpu.make_async_copy(result, output_out, store_sem.at[1])
    output_store.start()
    pltpu.make_async_copy(
        grad_in.at[pl.ds(0, slab - 1)], grad_in.at[pl.ds(0, slab - 1)], recv_sem.at[GRAD_A]
    ).wait()
    slab_sum[...] = jnp.sum(grad_in[...], axis=0)

    def along_z(i):
        z = lax.rem(my_z + i, n_z)
        remote(slab_sum, line_in.at[my_z], GRAD_B, (z * per_z + my_yc, rep))

    each(n_z, along_z)
    line_in[my_z] = slab_sum[...]
    pltpu.make_async_copy(
        line_in.at[pl.ds(0, n_z - 1)], line_in.at[pl.ds(0, n_z - 1)], recv_sem.at[GRAD_B]
    ).wait()
    total[...] = jnp.sum(line_in[...], axis=0)

    def spread_total(i):
        remote(total, grad_all.at[part_of(my_slab)], GRAD_C, slab_id(slab_peer(i)))

    each(slab, spread_total)
    grad_all[part_of(my_slab)] = total[...]
    pltpu.make_async_copy(
        grad_all.at[pl.ds(0, breadth - chunk)],
        grad_all.at[pl.ds(0, breadth - chunk)],
        recv_sem.at[GRAD_C],
    ).wait()
    grad_store = pltpu.make_async_copy(grad_all, grad_out, store_sem.at[2])
    grad_store.start()

    pltpu.make_async_copy(
        asked.at[pl.ds(0, n_dev - 1)], asked.at[pl.ds(0, n_dev - 1)], send_sem.at[REQ]
    ).wait()
    left(send_x, MIG_X)
    left(send_h, MIG_H)
    left(fetch_x, PULL_X)
    left(part_1, PUSH_1)
    left(fetch_h, PULL_H)
    left(part_2, PUSH_2)
    for stage in (GRAD_A, GRAD_C):
        pltpu.make_async_copy(
            grad.at[pl.ds(0, breadth - chunk)],
            grad.at[pl.ds(0, breadth - chunk)],
            send_sem.at[stage],
        ).wait()
    pltpu.make_async_copy(
        line_in.at[pl.ds(0, n_z - 1)], line_in.at[pl.ds(0, n_z - 1)], send_sem.at[GRAD_B]
    ).wait()
    hidden_store.wait()
    output_store.wait()
    grad_store.wait()


def body(
    n_dev,
    n_rep,
    n_y,
    n_core,
    features,
    history,
    new_owner,
    pull_rows,
    occupancy,
    adj_local,
    adj_boundary,
    w_first,
    bias_first,
    w_second,
    cotangent,
):
    rows, breadth = features.shape
    per_z = n_y * n_core
    slab = per_z * n_rep
    n_z = n_dev // per_z
    chunk = breadth // slab
    any_space = pl.BlockSpec(memory_space=pl.ANY)
    vmem = pl.BlockSpec(memory_space=pltpu.VMEM)
    wide = pltpu.VMEM((rows, breadth), BF16)
    square = pltpu.VMEM((rows, rows), BF16)
    hidden, output, grad = pl.pallas_call(
        functools.partial(step_kernel, n_dev, n_rep, n_y, n_core),
        name="gcn_step",
        out_shape=(
            jax.ShapeDtypeStruct((rows, breadth), BF16),
            jax.ShapeDtypeStruct((rows, breadth), BF16),
            jax.ShapeDtypeStruct((breadth, breadth), F32),
        ),
        in_specs=[any_space] * 2 + [vmem] * 3 + [any_space] * 3 + [vmem] + [any_space] * 2,
        out_specs=(any_space,) * 3,
        scratch_shapes=[
            wide,
            wide,
            square,
            square,
            square,
            pltpu.VMEM((breadth, breadth), BF16),
            pltpu.VMEM((breadth, breadth), BF16),
            wide,
            pltpu.VMEM((breadth, rows), BF16),
            wide,
            wide,
            wide,
            wide,
            pltpu.VMEM((n_dev, 1, 128), I32),
            pltpu.VMEM((n_dev, 128), I32),
            square,
            square,
            pltpu.VMEM((rows // 128, 2 * rows), F32),
            wide,
            wide,
            wide,
            wide,
            wide,
            wide,
            wide,
            wide,
            pltpu.VMEM((rows, breadth), F32),
            wide,
            wide,
            wide,
            pltpu.VMEM((breadth, breadth), F32),
            pltpu.VMEM((slab, chunk, breadth), F32),
            pltpu.VMEM((chunk, breadth), F32),
            pltpu.VMEM((n_z, chunk, breadth), F32),
            pltpu.VMEM((chunk, breadth), F32),
            pltpu.VMEM((breadth, breadth), F32),
            pltpu.SemaphoreType.DMA((7,)),
            pltpu.SemaphoreType.DMA((3,)),
            pltpu.SemaphoreType.DMA((10,)),
            pltpu.SemaphoreType.DMA((10,)),
        ],
        compiler_params=pltpu.CompilerParams(
            collective_id=0, has_side_effects=True, vmem_limit_bytes=60 * 2**20
        ),
    )(
        features,
        history,
        new_owner,
        pull_rows.reshape(rows // 128, 1, 128),
        occupancy,
        adj_local,
        adj_boundary,
        w_first,
        bias_first.reshape(1, breadth),
        w_second,
        cotangent,
    )
    return hidden, output, grad.T


def solution(mesh):
    split = P(("dev", "rep"), None)
    n_core, n_y = 2, 4
    return jax.shard_map(
        functools.partial(body, mesh.shape["dev"], mesh.shape["rep"], n_y, n_core),
        mesh=mesh,
        in_specs=(
            split,
            split,
            split,
            P(("dev", "rep")),
            split,
            split,
            split,
            P(),
            P(),
            P(),
            split,
        ),
        out_specs=(split, split, P()),
        check_vma=False,
    )
```

time: 209 us -> 111 us (0.53)
  Pallas kernels: 0 us -> 104 us
  waiting for transfers between devices: 79.8 us -> 0 us
  starting transfers between devices: 43.3 us -> 0 us
  blocking collectives: 36 us -> 0 us
  matrix products: 20.3 us -> 0 us
  local copies, waits for them, and re-layouts: 23.7 us -> 5.52 us
  other arithmetic: 4.08 us -> 0 us
    pallas_call x0 -> x1, Pallas kernels: none -> 104 us  [body(): pl.pallas_call(functools.partial(step_kernel, n_dev, n_rep, n_y, n_core),...]
    all_to_all x6 -> x0, waiting for transfers between devices: 79.8 us -> none  [the longest x2 44.7 us: in_one_piece(): lax.all_to_all(both, axis, split_axis=split_dim, concat_axis=concat_dim,...]
    all_to_all x6 -> x0, starting transfers between devices: 43.3 us -> none  [the longest x1 13.1 us: body(): lax.all_to_all(pull_rows.reshape(peer_count, per_peer), DEV, split_axis=0...]
    all_to_all x3 -> x0, blocking collectives: 36 us -> none  [the longest x1 13.4 us: summed_rows(): return jnp.sum(lax.all_to_all(own, far, 0, 0, tiled=True), axis=0)]
    dot_general x10 -> x0, matrix products: 20.3 us -> none  [the longest x2 5.94 us: dense_terms(): summed = jnp.dot(local_tile, owned, preferred_element_type=jnp.float32)]
    gather x4 -> x0, local copies, waits for them, and re-layouts: 10.1 us -> none  [the longest x2 7.88 us: fetch_rows(): return values[requests].reshape(peer_count, per_peer, breadth)]
    broadcast_in_dim x4 -> x0, local copies, waits for them, and re-layouts: 5.25 us -> none  [the longest x1 4.46 us: expand(): jnp.repeat(jnp.repeat(occupied, 128, axis=0), 128, axis=1)]
    all_to_all x3 -> x0, local copies, waits for them, and re-layouts: 2.8 us -> none  [the longest x2 1.95 us: body(): lax.all_to_all(pull_rows.reshape(peer_count, per_peer), DEV, split_axis=0...]
  transfers between devices with their start and end apart: 6 -> 0, of which waited for: 6 -> 0; matrix products, arithmetic and copies ran while one was open for 12% -> 0% of each run, Pallas kernels for 0% -> 0%
where the time goes in v1:
time: 111 us; the launch traced here: 110 us
  Pallas kernels  104 us (94%)
  local copies, waits for them, and re-layouts  5.52 us (5%)
    pallas_call x1, Pallas kernels, body(): pl.pallas_call(functools.partial(step_kernel, n_dev, n_rep, n_y, n_core),...  104 us
    unnamed x3, local copies, waits for them, and re-layouts  5.52 us

profile of v1, /device:TPU:1, one launch (start us, length us, event | category | flops | bytes accessed | tf_op | source)
XLA Modules:
  0.0 110.3 jit_solution(6718780528577395682)
XLA Ops:
  0.6 104.2 %gcn_step.1 = (bf16[1024,256]{1,0:T(8,128)(2,1)}, bf16[1024,256]{1,0:T(8,128)(2,1)}, f32[256,256]{1,0:T(8,128)}) custom-call(bf16[1024,256]{1,0:T(8,128)(2,1)} %features.1, bf16[1024,256]{1,0:T(8,128)(2,1)} %history.1, s32[1,64]{1,0:T(1,128)} %owner_ref.1, s32[8,1,128]{2,1,0:T(1,128)} %bitcast.4, s32[8,16]{1,0:T(8,128)} %occ_ref.1, ...), custom_call_target="tpu_custom_call" | custom-call | tf_op jit(solution)/shard_map/gcn_step/pallas_call | solution.py:410
  104.8 1.8 %copy.14 = f32[256,256]{1,0:T(8,128)} copy(f32[256,256]{0,1:T(8,128)} %bitcast.3) | data formatting | bytes 524288
  106.6 1.9 %copy.17 = bf16[1024,256]{1,0:T(8,128)(2,1)} copy(bf16[1024,256]{1,0:T(8,128)(2,1)} %get-tuple-element.15) | data formatting | bytes 1048576
  108.4 1.9 %copy.18 = bf16[1024,256]{1,0:T(8,128)(2,1)} copy(bf16[1024,256]{1,0:T(8,128)(2,1)} %get-tuple-element.16) | data formatting | bytes 1048576
